TPU v7x, 128 devices: a whole 4x4x4 slice. The times are simulated.
128 devices in a mesh: row: 8 (over y, x_lo), col: 16 (over x_hi, z, core).
Axes of the slice: x: 4 (x_hi: 2, x_lo: 2; x = x_hi * 2 + x_lo), y: 4, z: 4, core: 2. Of those that a mesh axis runs over, the one named last changes fastest.
Arguments:
- features: bfloat16 [131072, 128], P(('row', 'col')), may hold values from -24 to 24
- tile_rows: int32 [8, 16, 1024], P('row', 'col'), may hold values from 0 to 127
- tile_cols: int32 [8, 16, 1024], P('row', 'col'), may hold values from 0 to 63
- edge_lists: int32 [2, 8, 16, 1024, 128], P(None, 'row', 'col'), may hold values from -16 to 127
- tile_counts: int32 [8, 16], P('row', 'col'), may hold values from 128 to 1024, as said below
Outputs:
- hop_one: bfloat16 [131072, 128], P(('row', 'col'))
- hop_two: bfloat16 [131072, 128], P(('row', 'col'))
Inputs may be any that keep to these rules, and one draw needn't show every extreme that they name: `tile_counts`: live tile slots of a block; some block has exactly 1024. `edge_lists`: a negative entry marks an empty edge slot; slots at or past a block's count hold arbitrary entries. `tile_rows`: a tile may occur in several slots; slots at or past a block's count hold arbitrary entries. `tile_cols`: slots at or past a block's count hold arbitrary entries.
All inputs are finite; a program needn't handle non-finite values.
Results may differ from a plain program's by a relative error of at most 0.0058.
Values may be sent and summed in bfloat16 or wider, within the bound.
A program may use at most 192 MiB of HBM per device.

v0:
```python
import jax
import jax.numpy as jnp
from jax import lax
from jax.sharding import PartitionSpec as P

TILE = 128
GROUP = 32


def total_of_pieces(x, axis):
    return lax.all_gather(x, axis).astype(jnp.float32).sum(0)


def laid_out(pieces, dim):
    lengths = list(pieces.shape[1:])
    lengths[dim] *= pieces.shape[0]
    return jnp.moveaxis(pieces, 0, dim).reshape(lengths)


def sent_to_all(x, axis):
    size = lax.axis_size(axis)
    return lax.all_to_all(jnp.broadcast_to(x[None], (size, *x.shape)), axis, 0, 0, tiled=True)


def gathered_copies(x, axis, dim):
    return laid_out(sent_to_all(x, axis), dim)


def dense_tiles(dst_ids, src_ids):
    cell_ids = lax.broadcasted_iota(jnp.int32, (1, 1, TILE), 2)
    dst_hot = (dst_ids[:, :, None] == cell_ids).astype(jnp.bfloat16)
    src_hot = (src_ids[:, :, None] == cell_ids).astype(jnp.bfloat16)
    return jnp.einsum("geu,gev->guv", dst_hot, src_hot, preferred_element_type=jnp.float32).astype(
        jnp.bfloat16
    )


def group_turns(live_count):
    return (live_count + GROUP - 1) // GROUP


def alive_mask(start_slot, live_count):
    return (start_slot + lax.iota(jnp.int32, GROUP) < live_count).astype(jnp.float32)


def build_store(row_ids, dst_ids, src_ids, live_count, degree):

    def build_visit(turn_index, state_pair):
        tile_store, partial_degree = state_pair
        start_slot = turn_index * GROUP
        dense_group = dense_tiles(
            lax.dynamic_slice_in_dim(dst_ids, start_slot, GROUP, 0),
            lax.dynamic_slice_in_dim(src_ids, start_slot, GROUP, 0),
        )
        alive = alive_mask(start_slot, live_count)
        row_totals = jnp.sum(dense_group.astype(jnp.float32), axis=2) * alive[:, None]
        group_rows = lax.dynamic_slice_in_dim(row_ids, start_slot, GROUP, 0)
        partial_degree = partial_degree.at[group_rows].add(row_totals)
        tile_store = lax.dynamic_update_slice_in_dim(tile_store, dense_group, start_slot, 0)
        return (tile_store, partial_degree)

    empty = jnp.zeros((row_ids.shape[0], TILE, TILE), jnp.bfloat16)
    return lax.fori_loop(0, group_turns(live_count), build_visit, (empty, degree))


def apply_store(tile_store, row_ids, live_count, fetch, partial_value):

    def apply_visit(turn_index, summed):
        start_slot = turn_index * GROUP
        dense_group = lax.dynamic_slice_in_dim(tile_store, start_slot, GROUP, 0)
        product = jnp.einsum(
            "guv,gvf->guf", dense_group, fetch(start_slot), preferred_element_type=jnp.float32
        )
        alive = alive_mask(start_slot, live_count)
        group_rows = lax.dynamic_slice_in_dim(row_ids, start_slot, GROUP, 0)
        return summed.at[group_rows].add(product * alive[:, None, None])

    return lax.fori_loop(0, group_turns(live_count), apply_visit, partial_value)


def local(features, tile_rows, tile_cols, edge_lists, tile_counts):
    node_count, feat_width = features.shape
    col_size = lax.axis_size("col")
    block_tiles = node_count * col_size // TILE
    rows_own = tile_rows[0, 0]
    cols_own = tile_cols[0, 0]
    dst_own = edge_lists[0, 0, 0]
    src_own = edge_lists[1, 0, 0]
    tile_count = tile_counts[0, 0]
    degree = jnp.zeros((block_tiles, TILE), jnp.float32)
    store_own, degree = build_store(rows_own, dst_own, src_own, tile_count, degree)
    flat_degree = degree.reshape(-1)
    degree_all = total_of_pieces(flat_degree.astype(jnp.bfloat16), "col").astype(jnp.float32)
    own_degree = lax.dynamic_slice_in_dim(
        degree_all, lax.axis_index("col") * node_count, node_count, 0
    )
    inv_root = lax.rsqrt(1.0 + own_degree)

    def propagate(scaled):
        gathered = gathered_copies(scaled, "row", 0)
        sources = gathered.reshape(-1, TILE, feat_width)

        def fetch_own(start_slot):
            return sources[lax.dynamic_slice_in_dim(cols_own, start_slot, GROUP, 0)]

        partial_value = jnp.zeros((block_tiles, TILE, feat_width), jnp.float32)
        partial_value = apply_store(store_own, rows_own, tile_count, fetch_own, partial_value)
        flat_partial = partial_value.reshape(-1, feat_width)
        return lax.psum_scatter(flat_partial, "col", scatter_dimension=0, tiled=True)

    scaled_zero = (features.astype(jnp.float32) * inv_root[:, None]).astype(jnp.bfloat16)
    first_sum = propagate(scaled_zero)
    hop_one = (first_sum * inv_root[:, None]).astype(jnp.bfloat16)
    scaled_one = (first_sum * (inv_root * inv_root)[:, None]).astype(jnp.bfloat16)
    second_sum = propagate(scaled_one)
    hop_two = (second_sum * inv_root[:, None]).astype(jnp.bfloat16)
    return (hop_one, hop_two)


def solution(mesh):
    placed = (
        P(("row", "col"), None),
        P("row", "col", None),
        P("row", "col", None),
        P(None, "row", "col", None, None),
        P("row", "col"),
    )
    return jax.shard_map(
        local,
        mesh=mesh,
        in_specs=placed,
        out_specs=(P(("row", "col"), None), P(("row", "col"), None)),
        check_vma=False,
    )
```

profile of v0, /device:TPU:0, one launch (start us, length us, event | category | flops | bytes accessed | tf_op | source)
XLA Modules:
  0.0 1232.8 jit_solution(11944217096634722214)
XLA Ops:
  9.1 11.2 broadcast_in_dim.25.clone
  20.4 47.0 %while.32 = (s32[]{:T(128)}, bf16[1024,128,128]{2,1,0:T(8,128)(2,1)}, f32[128,128]{1,0:T(8,128)S(1)}, s32[]{:T(128)}, s32[1024,128]{1,0:T(8,128)S(1)}, /*index=5...) while((s32[]{:T(128)}, ...), condition=%wide.region_3.4_spmd, body=%wide.region_0.3_spmd.sunk | while | flops 136843456 | bytes 5440567 | solution.py:63
  67.4 60.9 %all-gather = bf16[16,1,16384]{2,1,0:T(2,128)(2,1)S(1)} all-gather(bf16[1,1,16384]{2,1,0:T(2,128)(2,1)S(1)} %reshape.93), channel_id=1, replica_groups=mesh['row'=8,'col'=16] {'col'}, dimensions={0}, use_global_device_ids=true | all-gather | bytes 557056 | tf_op jit(solution)/shard_map/all_gather | solution.py:11
  131.6 81.2 %all-to-all-start = ((bf16[8,1024,128]{2,1,0:T(8,128)(2,1)}), bf16[8,1024,128]{2,1,0:T(8,128)(2,1)}, u32[]{:S(2)}, u32[]{:S(2)}) async-start(bf16[8,1024,128]{2,1,0:T(8,128)(2,1)} %broadcast_in_dim.27), calls=%async_computation | async-start | bytes 4194304 | tf_op jit(solution)/shard_map/all_to_all | solution.py:22
  212.8 27.4 %all-to-all-done = bf16[8,1024,128]{2,1,0:T(8,128)(2,1)} async-done(((bf16[8,1024,128]{2,1,0:T(8,128)(2,1)}), bf16[8,1024,128]{2,1,0:T(8,128)(2,1)}, u32[]{:S(2)}, u32[]{:S(2)}) %all-to-all-start) | async-done | bytes 2097184 | tf_op jit(solution)/shard_map/all_to_all | solution.py:22
  240.2 4.3 broadcast.58.clone
  244.4 105.3 %while.33 = (s32[]{:T(128)}, f32[128,128,128]{2,1,0:T(8,128)}, s32[]{:T(128)}, s32[1024]{0:T(1024)}, bf16[1024,128,128]{2,1,0:T(8,128)(2,1)}, /*index=5*/s32[102...) while((s32[]{:T(128)}, f32[128,128,128]{2,1,0:T(8,128)}, ...), condition=%wide.region_7.8_spmd, body=%wide.region_5.7_spmd.sunk | while | flops 135267616 | bytes 12588339 | solution.py:78
  245.2 2.3 gather_fusion
  249.9 6.3 scatter_fusion
  257.0 2.3 gather_fusion
  261.6 6.2 scatter_fusion
  268.7 2.3 gather_fusion
  273.3 6.2 scatter_fusion
  280.4 2.3 gather_fusion
  285.0 6.2 scatter_fusion
  292.1 2.3 gather_fusion
  296.7 6.2 scatter_fusion
  303.7 2.3 gather_fusion
  308.4 6.2 scatter_fusion
  315.4 2.3 gather_fusion
  320.1 6.2 scatter_fusion
  327.0 2.3 gather_fusion
  331.7 6.3 scatter_fusion
  338.8 2.3 gather_fusion
  343.4 6.3 scatter_fusion
  349.8 367.3 %reduce-scatter.3.cloned.1.call-done = f32[1024,128]{1,0:T(8,128)} async-done(((f32[16384,128]{1,0:T(8,128)}), f32[1024,128]{1,0:T(8,128)}) %reduce-scatter.3.cloned.1.call-update) | async-done | bytes 524304 | tf_op jit(solution)/shard_map/reduce_scatter | solution.py:109
  720.7 4.4 all-to-all-start.1
  725.1 25.8 %all-to-all-done.1 = bf16[8,1024,128]{2,1,0:T(8,128)(2,1)} async-done(((bf16[8,1024,128]{2,1,0:T(8,128)(2,1)}), bf16[8,1024,128]{2,1,0:T(8,128)(2,1)}, u32[]{:S(2)}, u32[]{:S(2)}) %all-to-all-start.1) | async-done | bytes 2097184 | tf_op jit(solution)/shard_map/all_to_all | solution.py:22
  750.9 4.3 broadcast.58
  755.2 105.3 %while.34 = (s32[]{:T(128)}, f32[128,128,128]{2,1,0:T(8,128)}, s32[]{:T(128)}, s32[1024]{0:T(1024)}, bf16[1024,128,128]{2,1,0:T(8,128)(2,1)}, /*index=5*/s32[102...) while((s32[]{:T(128)}, f32[128,128,128]{2,1,0:T(8,128)}, ...), condition=%wide.region_11.12_spmd, body=%wide.region_9.11_spmd.sunk | while | flops 135267616 | bytes 12588339 | solution.py:78
  756.0 2.3 gather_fusion.1
  760.7 6.3 scatter_fusion.1
  767.7 2.3 gather_fusion.1
  772.4 6.2 scatter_fusion.1
  784.1 6.2 scatter_fusion.1
  791.2 2.3 gather_fusion.1
  795.8 6.2 scatter_fusion.1
  802.8 2.3 gather_fusion.1
  807.5 6.2 scatter_fusion.1
  814.5 2.3 gather_fusion.1
  819.2 6.2 scatter_fusion.1
  826.2 2.3 gather_fusion.1
  830.9 6.2 scatter_fusion.1
  837.8 2.3 gather_fusion.1
  842.5 6.3 scatter_fusion.1
  849.5 2.3 gather_fusion.1
  854.2 6.3 scatter_fusion.1
  860.5 363.4 %reduce-scatter.5.cloned.1.call-done = f32[1024,128]{1,0:T(8,128)} async-done(((f32[16384,128]{1,0:T(8,128)}), f32[1024,128]{1,0:T(8,128)}) %reduce-scatter.5.cloned.1.call-update) | async-done | bytes 524304 | tf_op jit(solution)/shard_map/reduce_scatter | solution.py:109
  (153 shorter events, 114.6 us)
Async XLA Ops:
  67.4 62.4 %copy-start = (bf16[1024,128]{1,0:T(8,128)(2,1)S(1)}, bf16[1024,128]{1,0:T(8,128)(2,1)}, u32[]{:S(2)}) copy-start(bf16[1024,128]{1,0:T(8,128)(2,1)} %param.11) | copy-start | bytes 786436
  131.6 108.6 %all-to-all-start = ((bf16[8,1024,128]{2,1,0:T(8,128)(2,1)}), bf16[8,1024,128]{2,1,0:T(8,128)(2,1)}, u32[]{:S(2)}, u32[]{:S(2)}) async-start(bf16[8,1024,128]{2,1,0:T(8,128)(2,1)} %broadcast_in_dim.27), calls=%async_computation | async-start | bytes 4194304 | tf_op jit(solution)/shard_map/all_to_all | solution.py:22
  212.8 504.3 %reduce-scatter.3.cloned.1.call-start = ((), (), s32[]{:S(2)}) async-start(), calls=%async_computation.4 | async-start | bytes 8912896 | tf_op jit(solution)/shard_map/reduce_scatter | solution.py:109
  720.7 30.3 %all-to-all-start.1 = ((bf16[8,1024,128]{2,1,0:T(8,128)(2,1)}), bf16[8,1024,128]{2,1,0:T(8,128)(2,1)}, u32[]{:S(2)}, u32[]{:S(2)}) async-start(bf16[8,1024,128]{2,1,0:T(8,128)(2,1)} %broadcast_in_dim.28), calls=%async_computation.2 | async-start | bytes 4194304 | tf_op jit(solution)/shard_map/all_to_all | solution.py:22
  725.0 498.9 %reduce-scatter.5.cloned.1.call-start = ((), (), s32[]{:S(2)}) async-start(), calls=%async_computation.5 | async-start | bytes 8912896 | tf_op jit(solution)/shard_map/reduce_scatter | solution.py:109
Sparse Core Ops, SparseCore 0:
  349.9 367.1 reduce-scatter.2
  860.7 363.2 reduce-scatter.4
where the time goes:
time: 1250 us; the launch traced here: 1230 us
  waiting for transfers between devices  784 us (63%)
  other arithmetic  164 us (13%)
  starting transfers between devices  85.6 us (7%)
  local copies, waits for them, and re-layouts  82.2 us (7%)
  blocking collectives  60.9 us (5%)
  matrix products  40.1 us (3%)
  between operations  14.8 us (1%)
    reduce_scatter x2, waiting for transfers between devices, propagate(): lax.psum_scatter(flat_partial, 'col', scatter_dimension=0, tiled=True)  731 us
    scatter-add x18, other arithmetic, apply_visit(): return summed.at[group_rows].add(product * alive[:, None, None])  112 us
    all_to_all x2, starting transfers between devices, sent_to_all(): lax.all_to_all(jnp.broadcast_to(x[None], (size, *x.shape)), axis, 0, 0, t...  85.6 us
    all_gather x1, blocking collectives, total_of_pieces(): return lax.all_gather(x, axis).astype(jnp.float32).sum(0)  60.9 us
    all_to_all x2, waiting for transfers between devices, sent_to_all(): lax.all_to_all(jnp.broadcast_to(x[None], (size, *x.shape)), axis, 0, 0, t...  53.2 us
    gather x18, local copies, waits for them, and re-layouts, fetch_own(): return sources[lax.dynamic_slice_in_dim(cols_own, start_slot, GROUP, 0)]  42.1 us
    dot_general x18, matrix products, apply_visit(): jnp.einsum('guv,gvf->guf', dense_group, fetch(start_slot), preferred_elem...  29.8 us
  transfers between devices with their start and end apart: 4, of which 4 were waited for; matrix products, arithmetic and copies ran while one was open for 0% of the time, Pallas kernels for 0%

commit v1 on v0

v1 whole, which is shorter than its diff:
```python
import functools

import jax
import jax.numpy as jnp
from jax import lax
from jax.experimental import pallas as pl
from jax.experimental.pallas import tpu as pltpu
from jax.sharding import PartitionSpec as P

TILE = 128
GROUP = 64
BATCH = 8


def last_group(count_ref):
    return (count_ref[0] - 1) // GROUP


def build_kernel(count_ref, rows_ref, dst_ref, src_ref, tiles_ref, degree_ref):
    group = pl.program_id(0)
    count = count_ref[0]

    @pl.when(group == 0)
    def _():
        degree_ref[...] = jnp.zeros_like(degree_ref)

    @pl.when(group * GROUP < count)
    def _():
        slot = group * GROUP + lax.broadcasted_iota(jnp.int32, (GROUP, TILE), 0)
        dst = jnp.where(slot < count, dst_ref[...], -1).astype(jnp.float32).astype(jnp.bfloat16)
        src = src_ref[...].astype(jnp.float32).astype(jnp.bfloat16)
        cell = lax.broadcasted_iota(jnp.int32, (TILE, TILE), 0).astype(jnp.float32).astype(jnp.bfloat16)
        one, zero = jnp.bfloat16(1), jnp.bfloat16(0)
        totals = []
        for i in range(GROUP):
            dst_hot = jnp.where(jnp.broadcast_to(dst[i : i + 1, :], (TILE, TILE)) == cell, one, zero)
            src_hot = jnp.where(jnp.broadcast_to(src[i : i + 1, :], (TILE, TILE)) == cell, one, zero)
            counts = lax.dot_general(
                src_hot, dst_hot, (((1,), (1,)), ((), ())), preferred_element_type=jnp.float32
            )
            tiles_ref[i] = counts.astype(jnp.bfloat16)
            totals.append(jnp.sum(counts, axis=0, keepdims=True))
        for i in range(GROUP):
            degree_ref[pl.ds(rows_ref[group * GROUP + i], 1), :] += totals[i]


def build_tiles(count, rows, dst, src):
    slots = dst.shape[0]
    lists = pl.BlockSpec((GROUP, TILE), lambda g, n, r: (jnp.minimum(g, last_group(n)), 0))
    return pl.pallas_call(
        build_kernel,
        grid_spec=pltpu.PrefetchScalarGridSpec(
            num_scalar_prefetch=2,
            grid=(slots // GROUP,),
            in_specs=[lists, lists],
            out_specs=[
                pl.BlockSpec((GROUP, TILE, TILE), lambda g, n, r: (jnp.minimum(g, last_group(n)), 0, 0)),
                pl.BlockSpec((TILE, TILE), lambda g, n, r: (0, 0)),
            ],
        ),
        out_shape=[
            jax.ShapeDtypeStruct((slots, TILE, TILE), jnp.bfloat16),
            jax.ShapeDtypeStruct((TILE, TILE), jnp.float32),
        ],
        name="build_tiles",
    )(count, rows, dst, src)


def apply_kernel(count_ref, rows_ref, cols_ref, tiles_ref, x_ref, out_ref, total):
    group = pl.program_id(0)

    @pl.when(group == 0)
    def _():
        total[...] = jnp.zeros_like(total)

    @pl.when(group * GROUP < count_ref[0])
    def _():
        base = group * GROUP
        for start in range(0, GROUP, BATCH):
            products = [
                jnp.dot(x_ref[cols_ref[base + i]], tiles_ref[i], preferred_element_type=jnp.float32)
                for i in range(start, start + BATCH)
            ]
            for j, product in enumerate(products):
                total[rows_ref[base + start + j]] += product

    @pl.when(group == pl.num_programs(0) - 1)
    def _():
        out_ref[...] = total[...].astype(jnp.bfloat16)


def apply_tiles(count, rows, cols, tiles, x):
    slots = tiles.shape[0]
    blocks = x.shape[0]
    return pl.pallas_call(
        apply_kernel,
        grid_spec=pltpu.PrefetchScalarGridSpec(
            num_scalar_prefetch=3,
            grid=(slots // GROUP,),
            in_specs=[
                pl.BlockSpec((GROUP, TILE, TILE), lambda g, n, r, c: (jnp.minimum(g, last_group(n)), 0, 0)),
                pl.BlockSpec((blocks, TILE, TILE), lambda g, n, r, c: (0, 0, 0)),
            ],
            out_specs=pl.BlockSpec((TILE, TILE, TILE), lambda g, n, r, c: (0, 0, 0)),
            scratch_shapes=[pltpu.VMEM((TILE, TILE, TILE), jnp.float32)],
        ),
        out_shape=jax.ShapeDtypeStruct((TILE, TILE, TILE), jnp.bfloat16),
        compiler_params=pltpu.CompilerParams(vmem_limit_bytes=40 * 2**20),
        name="apply_tiles",
    )(count, rows, cols, tiles, x)


def share_sum(partial, axis):
    size = lax.axis_size(axis)
    pieces = partial.reshape(size, partial.shape[0] // size, *partial.shape[1:])
    return lax.all_to_all(pieces, axis, 0, 0, tiled=True).astype(jnp.float32).sum(0)


def gathered(x, axis):
    size = lax.axis_size(axis)
    pieces = lax.all_to_all(jnp.broadcast_to(x[None], (size, *x.shape)), axis, 0, 0, tiled=True)
    return pieces.reshape(size * x.shape[0], *x.shape[1:])


def tile_transpose(x):
    return jnp.swapaxes(x, 1, 2)


def local(features, tile_rows, tile_cols, edge_lists, tile_counts):
    nodes, width = features.shape
    rows, cols = tile_rows[0, 0], tile_cols[0, 0]
    count = tile_counts[0]
    tiles, degree = build_tiles(count, rows, edge_lists[0, 0, 0], edge_lists[1, 0, 0])
    own_degree = share_sum(degree, "col")
    inv_root = lax.rsqrt(1.0 + own_degree)[:, None, :]

    def propagate(scaled):
        partial = apply_tiles(count, rows, cols, tiles, gathered(scaled, "row"))
        return share_sum(partial, "col")

    def output(x):
        return tile_transpose(x).reshape(nodes, width)

    own = tile_transpose(features.reshape(nodes // TILE, TILE, width))
    scaled_zero = (own.astype(jnp.float32) * inv_root).astype(jnp.bfloat16)
    first_sum = propagate(scaled_zero)
    hop_one = (first_sum * inv_root).astype(jnp.bfloat16)
    scaled_one = (first_sum * (inv_root * inv_root)).astype(jnp.bfloat16)
    second_sum = propagate(scaled_one)
    hop_two = (second_sum * inv_root).astype(jnp.bfloat16)
    return (output(hop_one), output(hop_two))


def solution(mesh):
    placed = (
        P(("row", "col"), None),
        P("row", "col", None),
        P("row", "col", None),
        P(None, "row", "col", None, None),
        P("row", "col"),
    )
    return jax.shard_map(
        local,
        mesh=mesh,
        in_specs=placed,
        out_specs=(P(("row", "col"), None), P(("row", "col"), None)),
        check_vma=False,
    )
```

time: 1250 us -> 279 us (0.22)
  the two profiles are of different devices: /device:TPU:0 before, /device:TPU:107 now
where the time goes in v1:
time: 279 us; the launch traced here: 277 us
  blocking collectives  148 us (53%)
  waiting for transfers between devices  61.7 us (22%)
  Pallas kernels  34.3 us (12%)
  starting transfers between devices  18.6 us (7%)
  local copies, waits for them, and re-layouts  7.1 us (3%)
  other arithmetic  5.07 us (2%)
    all_to_all x2, blocking collectives, share_sum(): lax.all_to_all(pieces, axis, 0, 0, tiled=True).astype(jnp.float32).sum(0)  91.6 us
    all_to_all x1, waiting for transfers between devices, share_sum(): lax.all_to_all(pieces, axis, 0, 0, tiled=True).astype(jnp.float32).sum(0)  61.7 us
    all_to_all x2, blocking collectives, gathered(): lax.all_to_all(jnp.broadcast_to(x[None], (size, *x.shape)), axis, 0, 0, t...  56.8 us
    pallas_call x2, Pallas kernels, apply_tiles(): pl.pallas_call(apply_kernel, grid_spec=pltpu.PrefetchScalarGridSpec(num_s...  21 us
    all_to_all x1, starting transfers between devices, share_sum(): lax.all_to_all(pieces, axis, 0, 0, tiled=True).astype(jnp.float32).sum(0)  18.6 us
    pallas_call x1, Pallas kernels, build_tiles(): pl.pallas_call(build_kernel, grid_spec=pltpu.PrefetchScalarGridSpec(num_s...  13.4 us
  transfers between devices with their start and end apart: 1, of which 1 were waited for; matrix products, arithmetic and copies ran while one was open for 0% of the time, Pallas kernels for 0%

profile of v1, /device:TPU:107, one launch (start us, length us, event | category | flops | bytes accessed | tf_op | source)
XLA Modules:
  0.0 276.6 jit_solution(7872455779944339657)
XLA Ops:
  1.3 2.3 slice_bitcast_fusion
  3.5 0.0 copy-start.1
  3.5 0.0 copy-start.2
  3.5 13.4 %build_tiles.1 = (bf16[1024,128,128]{2,1,0:T(8,128)(2,1)}, f32[128,128]{1,0:T(8,128)}) custom-call(s32[1]{0:T(128)} %bitcast.22.count_ref, s32[1024]{0:T(1024)} %bitcast.29, s32[1024,128]{1,0:T(8,128)} %get-tuple-element.7.dst_ref, s32[1024,128]{1,0:T(8,128)} %get-tuple-element.6.src_ref), custom_call_target="tpu_custom_call" | custom-call | tf_op jit(solution)/shard_map/build_tiles/pallas_call | solution.py:50
  16.9 24.3 %all_to_all.25 = f32[16,8,128]{2,1,0:T(8,128)S(1)} all-to-all(f32[16,8,128]{2,1,0:T(8,128)} %bitcast.37), channel_id=1, replica_groups=mesh['row'=8,'col'=16] {'col'}, dimensions={0} | all-to-all | bytes 131072 | tf_op jit(solution)/shard_map/all_to_all | solution.py:116
  41.2 1.2 fusion.3
  42.4 0.2 copy.10
  42.6 0.5 broadcast_in_dim.4
  43.1 28.4 %all_to_all.26 = bf16[8,8,128,128]{3,2,1,0:T(8,128)(2,1)S(1)} all-to-all(bf16[8,8,128,128]{3,2,1,0:T(8,128)(2,1)S(1)} %broadcast_in_dim.4), channel_id=1, replica_groups=mesh['row'=8,'col'=16] {'row'}, dimensions={0} | all-to-all | bytes 4194304 | tf_op jit(solution)/shard_map/all_to_all | solution.py:121
  71.4 0.0 copy-done.1
  71.5 0.0 copy-done.2
  71.5 10.5 %apply_tiles.2 = bf16[128,128,128]{2,1,0:T(8,128)(2,1)S(1)} custom-call(s32[1]{0:T(128)} %bitcast.23.count_ref, s32[1024]{0:T(1024)S(1)} %bitcast.30, s32[1024]{0:T(1024)S(1)} %bitcast.32, bf16[1024,128,128]{2,1,0:T(8,128)(2,1)} %get-tuple-element.4.tiles_ref, bf16[64,128,128]{2,1,0:T(8,128)(2,1)S(1)} %bitcast.28), custom_call_target="tpu_custom_call" | custom-call | tf_op jit(solution)/shard_map/apply_tiles/pallas_call | solution.py:95
  81.9 67.3 %all_to_all.27 = bf16[16,8,128,128]{3,2,1,0:T(8,128)(2,1)S(1)} all-to-all(bf16[16,8,128,128]{3,2,1,0:T(8,128)(2,1)S(1)} %bitcast.26), channel_id=1, replica_groups=mesh['row'=8,'col'=16] {'col'}, dimensions={0} | all-to-all | bytes 8388608 | tf_op jit(solution)/shard_map/all_to_all | solution.py:116
  149.3 0.8 convert_reduce_fusion.1
  150.0 0.1 multiply_convert_fusion.1
  150.1 0.5 broadcast_in_dim.5
  150.6 28.4 %all_to_all.28 = bf16[8,8,128,128]{3,2,1,0:T(8,128)(2,1)S(1)} all-to-all(bf16[8,8,128,128]{3,2,1,0:T(8,128)(2,1)S(1)} %broadcast_in_dim.5), channel_id=1, replica_groups=mesh['row'=8,'col'=16] {'row'}, dimensions={0} | all-to-all | bytes 4194304 | tf_op jit(solution)/shard_map/all_to_all | solution.py:121
  179.1 10.5 %apply_tiles.3 = bf16[128,128,128]{2,1,0:T(8,128)(2,1)S(1)} custom-call(s32[1]{0:T(128)} %bitcast.24.count_ref, s32[1024]{0:T(1024)S(1)} %bitcast.31, s32[1024]{0:T(1024)S(1)} %bitcast.33, bf16[1024,128,128]{2,1,0:T(8,128)(2,1)} %get-tuple-element.4.tiles_ref, bf16[64,128,128]{2,1,0:T(8,128)(2,1)S(1)} %bitcast.27), custom_call_target="tpu_custom_call" | custom-call | tf_op jit(solution)/shard_map/apply_tiles/pallas_call | solution.py:95
  189.6 0.0 copy-start
  189.6 2.0 copy-done
  191.5 18.6 %all-to-all-start.4 = ((bf16[16,8,128,128]{3,2,1,0:T(8,128)(2,1)}), bf16[16,8,128,128]{3,2,1,0:T(8,128)(2,1)}, u32[]{:S(2)}, u32[]{:S(2)}) async-start(bf16[16,8,128,128]{3,2,1,0:T(8,128)(2,1)} %bitcast.25), calls=%async_computation.4 | async-start | bytes 8388608 | tf_op jit(solution)/shard_map/all_to_all | solution.py:116
  210.1 0.9 copy.11
  211.0 61.7 %all-to-all-done.4 = bf16[16,8,128,128]{3,2,1,0:T(8,128)(2,1)} async-done(((bf16[16,8,128,128]{3,2,1,0:T(8,128)(2,1)}), bf16[16,8,128,128]{3,2,1,0:T(8,128)(2,1)}, u32[]{:S(2)}, u32[]{:S(2)}) %all-to-all-start.4) | async-done | bytes 4194336 | tf_op jit(solution)/shard_map/all_to_all | solution.py:116
  272.7 3.0 %convert_reduce_fusion = f32[8,128,128]{2,1,0:T(8,128)S(1)} fusion(bf16[16,8,128,128]{3,2,1,0:T(8,128)(2,1)} %all-to-all-done.4), kind=kLoop, calls=%fused_computation | loop fusion | flops 4063232 | bytes 4718592 | tf_op jit(solution)/shard_map/reduce_sum | solution.py:116
  275.7 0.9 copy.12
  (3 shorter events, 0.1 us)
Async XLA Ops:
  3.5 67.9 %copy-start.1 = (s32[1,1,1024]{2,1,0:T(1,128)S(1)}, s32[1,1,1024]{2,1,0:T(1,128)}, u32[]{:S(2)}) copy-start(s32[1,1,1024]{2,1,0:T(1,128)} %param.6) | copy-start | bytes 12292
  3.5 67.9 %copy-start.2 = (s32[1,1,1024]{2,1,0:T(1,128)S(1)}, s32[1,1,1024]{2,1,0:T(1,128)}, u32[]{:S(2)}) copy-start(s32[1,1,1024]{2,1,0:T(1,128)} %param.7) | copy-start | bytes 12292
  189.6 2.0 copy-start
  191.5 81.1 %all-to-all-start.4 = ((bf16[16,8,128,128]{3,2,1,0:T(8,128)(2,1)}), bf16[16,8,128,128]{3,2,1,0:T(8,128)(2,1)}, u32[]{:S(2)}, u32[]{:S(2)}) async-start(bf16[16,8,128,128]{3,2,1,0:T(8,128)(2,1)} %bitcast.25), calls=%async_computation.4 | async-start | bytes 8388608 | tf_op jit(solution)/shard_map/all_to_all | solution.py:116
